TPU v7x, 32 devices: a whole 2x2x4 slice. The times are simulated.
32 devices in a mesh: rows: 16 (over z, y, x), sub: 2 (over core).
Axes of the slice: x: 2, y: 2, z: 4, core: 2. Of those that a mesh axis runs over, the one named last changes fastest.
Arguments:
- matrix: float32 [4096, 384], P(('rows', 'sub')), as said below
- grad_out: float32 [4096, 384], P(('rows', 'sub')), as said below
- grad_factor: float32 [384, 384], replicated, may hold values from -6 to 6
Outputs:
- grad_matrix: float32 [4096, 384], P(('rows', 'sub'))
Inputs may be any that keep to these rules, and one draw needn't show every extreme that they name: `matrix`: entries at most of order 1 / sqrt(4096), with a scale that varies by row and by column. `grad_out`: entries of order 0.01.
All inputs are finite; a program needn't handle non-finite values.
Results may differ from a plain program's by a relative error of at most 0.0004.
Values sent between devices are 32-bit elements; how exact they have to be, the bound alone decides.
No kernel may reach another device: no remote copies, remote signals or barrier semaphores. Data moves between devices by JAX's collectives and lax.ppermute only.
A program may use at most 64 MiB of HBM per device.

v0:
```python
import jax
import jax.numpy as jnp
from jax import lax
from jax.sharding import PartitionSpec as P

SECTIONS = 2
shift_frac = 0.02


def full_dot(left, right):
    return jnp.dot(left, right, precision=lax.Precision.HIGHEST, preferred_element_type=jnp.float32)


def inner_gram(left, right):
    return lax.dot_general(
        left,
        right,
        (((0,), (0,)), ((), ())),
        precision=lax.Precision.HIGHEST,
        preferred_element_type=jnp.float32,
    )


def cholesky_adjoint(lower_fac, lower_inv, lower_grad):
    product = full_dot(lower_fac.T, lower_grad)
    phi_part = jnp.tril(product) - 0.5 * jnp.diag(jnp.diag(product))
    sandwich = full_dot(full_dot(lower_inv.T, phi_part), lower_inv)
    return 0.5 * (sandwich + sandwich.T)


def factor_grads(uppers, grad_factor):
    count = len(uppers)
    result = []
    for section_index in range(count):
        middle = grad_factor
        for later in range(section_index + 1, count):
            middle = full_dot(uppers[later].T, middle)
        for earlier in range(section_index - 1, -1, -1):
            middle = full_dot(middle, uppers[earlier].T)
        result.append(middle)
    return result


def summed_gram(partial_value):
    half_rows = lax.psum_scatter(partial_value, "sub", scatter_dimension=0, tiled=True)
    half_rows = lax.psum(half_rows, "rows")
    return lax.all_gather(half_rows, "sub", axis=0, tiled=True)


def per_device(matrix, grad_out, grad_factor):
    width = matrix.shape[1]
    rate = shift_frac / width
    identity = jnp.eye(width, dtype=jnp.float32)
    current = matrix
    saved = []
    for section_index in range(SECTIONS):
        summed = summed_gram(inner_gram(current, current))
        shift_val = rate * jnp.trace(summed)
        lower_fac = jnp.linalg.cholesky(summed + shift_val * identity)
        lower_inv = lax.linalg.triangular_solve(lower_fac, identity, left_side=True, lower=True)
        following = full_dot(current, lower_inv.T)
        saved.append((current, following, lower_fac, lower_inv))
        current = following
    uppers = [item[2].T for item in saved]
    fac_grads = factor_grads(uppers, grad_factor)
    q_grad = grad_out
    for section_index in range(SECTIONS - 1, -1, -1):
        before, after, lower_fac, lower_inv = saved[section_index]
        crossed = lax.psum(inner_gram(after, q_grad), ("rows", "sub"))
        total_grad = fac_grads[section_index] - full_dot(crossed, lower_inv)
        gram_grad = cholesky_adjoint(lower_fac, lower_inv, jnp.tril(total_grad.T))
        gram_grad = gram_grad + rate * jnp.trace(gram_grad) * identity
        q_grad = full_dot(q_grad, lower_inv) + 2.0 * full_dot(before, gram_grad)
    return q_grad


def solution(mesh):
    placed = (P(("rows", "sub"), None), P(("rows", "sub"), None), P())
    return jax.shard_map(
        per_device, mesh=mesh, in_specs=placed, out_specs=P(("rows", "sub"), None), check_vma=False
    )
```

profile of v0, /device:TPU:0, one launch (start us, length us, event | category | flops | bytes accessed | tf_op | source)
XLA Modules:
  0.0 777.9 jit_solution(7228258176599560391)
XLA Ops:
  6.5 2.6 fusion.120
  9.2 11.2 %reduce-scatter.7.cloned.1.call-done = f32[192,384]{1,0:T(8,128)} async-done(((f32[384,384]{1,0:T(8,128)}), f32[192,384]{1,0:T(8,128)}) %reduce-scatter.7.cloned.1.call-update) | async-done | bytes 294928
  20.3 1.9 copy.59
  22.4 113.0 %all-reduce.6.cloned.1.call-done = f32[192,384]{0,1:T(8,128)} async-done(((f32[192,384]{0,1:T(8,128)}), f32[192,384]{0,1:T(8,128)}) %all-reduce.6.cloned.1.call-update) | async-done | bytes 294928 | tf_op jit(solution)/shard_map/psum | solution.py:46
  135.3 1.1 copy.25
  136.5 2.2 all_gather.6
  140.5 11.7 %cholesky.208 = f32[128,128]{1,0:T(8,128)S(1)} custom-call(f32[128,128]{1,0:T(8,128)S(1)} %cholesky.310), custom_call_target="Cholesky" | custom-call | tf_op jit(solution)/shard_map/jit(cholesky)/cholesky | solution.py:59
  152.3 9.8 %custom-call.24 = f32[1,128,128]{1,2,0:T(8,128)S(1)} custom-call(f32[1,128,128]{2,1,0:T(8,128)S(1)} %get-tuple-element.56), custom_call_target="InvertDiagBlocksLowerTriangular" | custom-call | tf_op jit(solution)/shard_map/jit(cholesky)/cholesky | solution.py:59
  162.7 11.7 %cholesky.227 = f32[128,128]{1,0:T(8,128)S(1)} custom-call(f32[128,128]{1,0:T(8,128)S(1)} %cholesky.314), custom_call_target="Cholesky" | custom-call | tf_op jit(solution)/shard_map/jit(cholesky)/cholesky | solution.py:59
  174.5 10.0 %custom-call.25 = f32[1,128,128]{1,2,0:T(8,128)S(1)} custom-call(f32[1,128,128]{2,1,0:T(8,128)S(1)} %get-tuple-element.53), custom_call_target="InvertDiagBlocksLowerTriangular" | custom-call | tf_op jit(solution)/shard_map/jit(cholesky)/cholesky | solution.py:59
  184.9 11.7 %cholesky.246 = f32[128,128]{1,0:T(8,128)S(1)} custom-call(f32[128,128]{1,0:T(8,128)S(1)} %convolution_subtract_fusion.9), custom_call_target="Cholesky" | custom-call | tf_op jit(solution)/shard_map/jit(cholesky)/cholesky | solution.py:59
  200.0 6.0 while.4
  200.7 1.3 bitcast_dynamic-update-slice_fusion.4
  202.7 1.3 bitcast_dynamic-update-slice_fusion.4
  204.7 1.3 bitcast_dynamic-update-slice_fusion.4
  206.0 29.5 %custom-call.26 = f32[3,128,128]{1,2,0:T(8,128)S(1)} custom-call(f32[3,128,128]{2,1,0:T(8,128)S(1)} %get-tuple-element.21), custom_call_target="InvertDiagBlocksLowerTriangular" | custom-call | tf_op jit(solution)/shard_map/triangular_solve/custom-call.2 | solution.py:60
  236.8 0.8 convolution_subtract_fusion.4
  239.2 1.4 fusion.121
  240.7 7.1 reduce-scatter.9.cloned.1.call-done
  247.8 1.9 copy.61
  249.8 112.9 %all-reduce.8.cloned.1.call-done = f32[192,384]{0,1:T(8,128)} async-done(((f32[192,384]{0,1:T(8,128)}), f32[192,384]{0,1:T(8,128)}) %all-reduce.8.cloned.1.call-update) | async-done | bytes 294928 | tf_op jit(solution)/shard_map/psum | solution.py:46
  362.7 1.1 copy.32
  363.8 2.4 all_gather.7
  367.8 1.0 copy.35
  368.8 1.1 fusion.6
  370.0 11.7 %cholesky.261 = f32[128,128]{1,0:T(8,128)S(1)} custom-call(f32[128,128]{1,0:T(8,128)S(1)} %cholesky.318), custom_call_target="Cholesky" | custom-call | tf_op jit(solution)/shard_map/jit(cholesky)/cholesky | solution.py:59
  381.8 9.8 %custom-call.27 = f32[1,128,128]{1,2,0:T(8,128)S(1)} custom-call(f32[1,128,128]{2,1,0:T(8,128)S(1)} %get-tuple-element.49), custom_call_target="InvertDiagBlocksLowerTriangular" | custom-call | tf_op jit(solution)/shard_map/jit(cholesky)/cholesky | solution.py:59
  392.2 11.7 %cholesky.280 = f32[128,128]{1,0:T(8,128)S(1)} custom-call(f32[128,128]{1,0:T(8,128)S(1)} %cholesky.322), custom_call_target="Cholesky" | custom-call | tf_op jit(solution)/shard_map/jit(cholesky)/cholesky | solution.py:59
  405.3 10.2 %custom-call.28 = f32[1,128,128]{1,2,0:T(8,128)S(1)} custom-call(f32[1,128,128]{2,1,0:T(8,128)S(1)} %get-tuple-element.46), custom_call_target="InvertDiagBlocksLowerTriangular" | custom-call | tf_op jit(solution)/shard_map/jit(cholesky)/cholesky | solution.py:59
  416.0 11.7 %cholesky.299 = f32[128,128]{1,0:T(8,128)S(1)} custom-call(f32[128,128]{1,0:T(8,128)S(1)} %convolution_subtract_fusion.8), custom_call_target="Cholesky" | custom-call | tf_op jit(solution)/shard_map/jit(cholesky)/cholesky | solution.py:59
  430.4 0.9 fusion.11
  431.3 8.7 %while.5 = (s32[]{:T(128)}, f32[384,384]{1,0:T(8,128)}, s32[3,2]{0,1:T(2,128)S(1)}, f32[3,128,128]{2,1,0:T(8,128)S(1)}, s32[]{:T(128)}) while((s32[]{:T(128)}, f32[384,384]{1,0:T(8,128)}, s32[3,2]{0,1:T(2,128)S(1)}, f32[3,128,128]{2,1,0:T(8,128)S(1)}, s32[]{:T(128)}) %tuple.65), condition=%wide.while_cond.clone, body=%wide.while_body.clone.sunk | while | flops 2 | bytes 131181 | solution.py:60
  431.9 2.2 bitcast_dynamic-update-slice_fusion.5
  434.8 2.2 bitcast_dynamic-update-slice_fusion.5
  437.8 2.2 bitcast_dynamic-update-slice_fusion.5
  439.9 29.5 %custom-call.29 = f32[3,128,128]{1,2,0:T(8,128)S(1)} custom-call(f32[3,128,128]{2,1,0:T(8,128)S(1)} %get-tuple-element.22), custom_call_target="InvertDiagBlocksLowerTriangular" | custom-call | tf_op jit(solution)/shard_map/triangular_solve/custom-call.2 | solution.py:60
  470.1 1.3 convolution_subtract_fusion.3
  471.5 1.2 fusion.78
  472.7 1.7 convolution_subtract_fusion.2
  474.4 1.2 fusion.76
  475.7 0.8 fusion.115
  476.7 1.5 fusion.122
  478.5 2.1 fusion.38
  480.6 125.3 %all-reduce.10.cloned.1.call-done = f32[384,384]{1,0:T(8,128)} async-done(((f32[384,384]{1,0:T(8,128)}), f32[384,384]{1,0:T(8,128)}) %all-reduce.10.cloned.1.call-update) | async-done | bytes 589840 | tf_op jit(solution)/shard_map/psum | solution.py:69
  605.9 2.5 fusion
  608.4 1.5 fusion.34
  609.9 1.0 copy.40
  611.0 3.4 gather_fusion
  614.4 3.3 fusion.21
  617.7 1.3 fusion.114
  619.0 1.0 copy.41
  620.0 1.7 select_reduce_fusion.1
  622.4 1.8 convolution_multiply_fusion.1
  624.2 1.1 fusion.3
  625.3 1.4 fusion.123
  626.8 1.3 convolution_bitcast_fusion
  628.1 127.6 %all-reduce.12.cloned.1.call-done = f32[384,384]{1,0:T(8,128)} async-done(((f32[384,384]{1,0:T(8,128)}), f32[384,384]{1,0:T(8,128)}) %all-reduce.12.cloned.1.call-update) | async-done | bytes 589840 | tf_op jit(solution)/shard_map/psum | solution.py:69
  755.7 2.4 fusion.1
  758.1 1.5 fusion.36
  759.8 3.7 gather_fusion.1
  763.5 2.1 fusion.14
  765.6 1.3 fusion.116
  768.6 0.8 fusion.2
  769.5 1.3 convolution_add_fusion
  (103 shorter events, 17.5 us)
Async XLA Ops:
  6.5 471.9 %copy-start = (f32[384,384]{1,0:T(8,128)S(1)}, f32[384,384]{1,0:T(8,128)}, u32[]{:S(2)}) copy-start(f32[384,384]{1,0:T(8,128)} %param.8) | copy-start | bytes 1769476
  6.5 13.8 %reduce-scatter.7.cloned.1.call-start = ((), (), s32[]{:S(2)}) async-start(), calls=%async_computation.6 | async-start | bytes 884736
  9.1 126.2 %all-reduce.6.cloned.1.call-start = ((), (), s32[]{:S(2)}) async-start(), calls=%async_computation.2 | async-start | bytes 786432 | tf_op jit(solution)/shard_map/psum | solution.py:46
  22.2 225.6 %reduce-scatter.9.cloned.1.call-start = ((), (), s32[]{:S(2)}) async-start(), calls=%async_computation.7 | async-start | bytes 884736
  22.3 214.5 %copy-start.1 = (f32[384,384]{0,1:T(8,128)}, f32[384,384]{0,1:T(8,128)S(1)}, u32[]{:S(2)}) copy-start(f32[384,384]{0,1:T(8,128)S(1)} %fusion.26) | copy-start | bytes 1769476
  237.6 0.9 copy-start.6
  240.7 122.0 %all-reduce.8.cloned.1.call-start = ((), (), s32[]{:S(2)}) async-start(), calls=%async_computation.3 | async-start | bytes 786432 | tf_op jit(solution)/shard_map/psum | solution.py:46
  249.7 356.1 %all-reduce.10.cloned.1.call-start = ((), (), s32[]{:S(2)}) async-start(), calls=%async_computation.4 | async-start | bytes 1179648 | tf_op jit(solution)/shard_map/psum | solution.py:69
  370.0 11.7 %copy-start.10 = (f32[384,384]{1,0:T(8,128)}, f32[384,384]{1,0:T(8,128)S(1)}, u32[]{:S(2)}) copy-start(f32[384,384]{1,0:T(8,128)S(1)} %fusion.6) | copy-start | bytes 1769476
  381.7 9.9 %copy-start.11 = (f32[384,384]{1,0:T(8,128)S(1)}, f32[384,384]{1,0:T(8,128)}, u32[]{:S(2)}) copy-start(f32[384,384]{1,0:T(8,128)} %copy-done.10) | copy-start | bytes 1769476
  430.4 39.1 %copy-start.2 = (f32[384,384]{0,1:T(8,128)S(1)}, f32[384,384]{0,1:T(8,128)}, u32[]{:S(2)}) copy-start(f32[384,384]{0,1:T(8,128)} %copy-done.1) | copy-start | bytes 1769476
  469.5 0.7 copy-start.14
  475.7 130.2 %copy-start.3 = (f32[128,384]{1,0:T(8,128)}, f32[128,384]{1,0:T(8,128)S(1)}, u32[]{:S(2)}) copy-start(f32[128,384]{1,0:T(8,128)S(1)} %fusion.76) | copy-start | bytes 589828
  475.7 1.0 copy-start.12
  478.2 277.5 %all-reduce.12.cloned.1.call-start = ((), (), s32[]{:S(2)}) async-start(), calls=%async_computation.5 | async-start | bytes 1179648 | tf_op jit(solution)/shard_map/psum | solution.py:69
  614.4 3.3 copy-start.4
  622.3 1.8 copy-start.5
  622.3 1.8 copy-start.13
  625.3 1.5 copy-start.8
  767.1 1.4 copy-start.7
  768.5 0.9 copy-start.9
Sparse Core Ops, SparseCore 0:
  9.6 10.6 reduce-scatter.6
  25.5 109.7 all-reduce.5
  240.8 6.9 reduce-scatter.8
  252.9 109.7 all-reduce.7
  478.4 127.4 all-reduce.9
  626.9 128.7 all-reduce.11
where the time goes:
time: 788 us; the launch traced here: 778 us
  waiting for transfers between devices  497 us (63%)
  other arithmetic  179 us (23%)
  matrix products  43.1 us (5%)
  local copies, waits for them, and re-layouts  33.2 us (4%)
  between operations  20.5 us (3%)
    psum x2, waiting for transfers between devices, per_device(): crossed = lax.psum(inner_gram(after, q_grad), ('rows', 'sub'))  253 us
    psum x2, waiting for transfers between devices, summed_gram(): half_rows = lax.psum(half_rows, 'rows')  226 us
    another operation x21, other arithmetic, per_device(): lower_fac = jnp.linalg.cholesky(summed + shift_val * identity)  114 us
    another operation x5, other arithmetic, per_device(): lax.linalg.triangular_solve(lower_fac, identity, left_side=True, lower=True)  59.9 us
    dot_general x16, matrix products, full_dot(): jnp.dot(left, right, precision=lax.Precision.HIGHEST, preferred_element_t...  25.7 us
    unnamed x8, waiting for transfers between devices  18.4 us
  transfers between devices with their start and end apart: 6, of which 6 were waited for; matrix products, arithmetic and copies ran while one was open for 0% of the time, Pallas kernels for 0%

commit v1 on v0

--- a/solution.py
+++ b/solution.py
@@ -43,7 +43,8 @@
 
 def summed_gram(partial_value):
     half_rows = lax.psum_scatter(partial_value, "sub", scatter_dimension=0, tiled=True)
-    half_rows = lax.psum(half_rows, "rows")
+    pieces = lax.all_gather(half_rows, "rows")
+    half_rows = jnp.sum(pieces, axis=0)
     return lax.all_gather(half_rows, "sub", axis=0, tiled=True)
 
 

time: 788 us -> 740 us (0.939)
  waiting for transfers between devices: 497 us -> 438 us
  matrix products: 43.1 us -> 51.1 us
    psum x2 -> x0, waiting for transfers between devices: 226 us -> none  [summed_gram(): half_rows = lax.psum(half_rows, 'rows')]
    all_gather x0 -> x2, waiting for transfers between devices: none -> 167 us  [summed_gram(): pieces = lax.all_gather(half_rows, 'rows')]
    unnamed x8 -> x6, waiting for transfers between devices: 18.4 us -> 0.1 us
    reduce_scatter x0 -> x2, waiting for transfers between devices: none -> 17.9 us  [summed_gram(): lax.psum_scatter(partial_value, 'sub', scatter_dimension=0, tiled=True)]
where the time goes in v1:
time: 740 us; the launch traced here: 729 us
  waiting for transfers between devices  438 us (59%)
  other arithmetic  185 us (25%)
  matrix products  51.1 us (7%)
  local copies, waits for them, and re-layouts  30.2 us (4%)
  between operations  20.6 us (3%)
    psum x2, waiting for transfers between devices, per_device(): crossed = lax.psum(inner_gram(after, q_grad), ('rows', 'sub'))  253 us
    all_gather x2, waiting for transfers between devices, summed_gram(): pieces = lax.all_gather(half_rows, 'rows')  167 us
    another operation x21, other arithmetic, per_device(): lower_fac = jnp.linalg.cholesky(summed + shift_val * identity)  114 us
    another operation x5, other arithmetic, per_device(): lax.linalg.triangular_solve(lower_fac, identity, left_side=True, lower=True)  59.9 us
    dot_general x16, matrix products, full_dot(): jnp.dot(left, right, precision=lax.Precision.HIGHEST, preferred_element_t...  27.4 us
    reduce_scatter x2, waiting for transfers between devices, summed_gram(): lax.psum_scatter(partial_value, 'sub', scatter_dimension=0, tiled=True)  17.9 us
  transfers between devices with their start and end apart: 6, of which 6 were waited for; matrix products, arithmetic and copies ran while one was open for 0% of the time, Pallas kernels for 0%

profile of v1, /device:TPU:0, one launch (start us, length us, event | category | flops | bytes accessed | tf_op | source)
XLA Modules:
  0.0 729.5 jit_solution(6322254099449447524)
XLA Ops:
  6.5 2.6 fusion.120
  9.2 11.2 %reduce-scatter.3.cloned.1.call-done = f32[192,384]{1,0:T(8,128)} async-done(((f32[384,384]{1,0:T(8,128)}), f32[192,384]{1,0:T(8,128)}) %reduce-scatter.3.cloned.1.call-update) | async-done | bytes 294928 | tf_op jit(solution)/shard_map/reduce_scatter | solution.py:45
  20.5 83.5 %all-gather.5.cloned.1.call-done = f32[3072,384]{1,0:T(8,128)} async-done(((f32[192,384]{1,0:T(8,128)}), f32[3072,384]{1,0:T(8,128)}) %all-gather.5.cloned.1.call-update) | async-done | bytes 4718608 | tf_op jit(solution)/shard_map/all_gather | solution.py:46
  104.0 2.6 reduce_sum.37
  106.6 2.2 all_gather.20
  111.6 11.7 %cholesky.208 = f32[128,128]{1,0:T(8,128)S(1)} custom-call(f32[128,128]{1,0:T(8,128)S(1)} %cholesky.310), custom_call_target="Cholesky" | custom-call | tf_op jit(solution)/shard_map/jit(cholesky)/cholesky | solution.py:60
  123.4 9.8 %custom-call.24 = f32[1,128,128]{1,2,0:T(8,128)S(1)} custom-call(f32[1,128,128]{2,1,0:T(8,128)S(1)} %get-tuple-element.56), custom_call_target="InvertDiagBlocksLowerTriangular" | custom-call | tf_op jit(solution)/shard_map/jit(cholesky)/cholesky | solution.py:60
  133.3 1.2 constant_dynamic-update-slice_fusion.3
  134.4 1.2 convolution_subtract_fusion.7
  135.6 11.7 %cholesky.227 = f32[128,128]{1,0:T(8,128)S(1)} custom-call(f32[128,128]{1,0:T(8,128)S(1)} %cholesky.314), custom_call_target="Cholesky" | custom-call | tf_op jit(solution)/shard_map/jit(cholesky)/cholesky | solution.py:60
  147.4 10.0 %custom-call.25 = f32[1,128,128]{1,2,0:T(8,128)S(1)} custom-call(f32[1,128,128]{2,1,0:T(8,128)S(1)} %get-tuple-element.53), custom_call_target="InvertDiagBlocksLowerTriangular" | custom-call | tf_op jit(solution)/shard_map/jit(cholesky)/cholesky | solution.py:60
  157.6 1.1 convolution_subtract_fusion.9
  158.7 11.7 %cholesky.246 = f32[128,128]{1,0:T(8,128)S(1)} custom-call(f32[128,128]{1,0:T(8,128)S(1)} %convolution_subtract_fusion.9), custom_call_target="Cholesky" | custom-call | tf_op jit(solution)/shard_map/jit(cholesky)/cholesky | solution.py:60
  173.8 6.1 while.4
  174.5 1.3 bitcast_dynamic-update-slice_fusion.4
  176.5 1.3 bitcast_dynamic-update-slice_fusion.4
  178.6 1.3 bitcast_dynamic-update-slice_fusion.4
  179.9 29.5 %custom-call.26 = f32[3,128,128]{1,2,0:T(8,128)S(1)} custom-call(f32[3,128,128]{2,1,0:T(8,128)S(1)} %get-tuple-element.21), custom_call_target="InvertDiagBlocksLowerTriangular" | custom-call | tf_op jit(solution)/shard_map/triangular_solve/custom-call.2 | solution.py:61
  212.6 1.4 fusion.121
  214.1 6.8 reduce-scatter.5.cloned.1.call-done
  220.9 83.4 %all-gather.7.cloned.1.call-done = f32[3072,384]{1,0:T(8,128)} async-done(((f32[192,384]{1,0:T(8,128)}), f32[3072,384]{1,0:T(8,128)}) %all-gather.7.cloned.1.call-update) | async-done | bytes 4718608 | tf_op jit(solution)/shard_map/all_gather | solution.py:46
  304.4 2.6 reduce_sum.48
  306.9 2.6 all_gather.23
  309.5 1.3 copy.26
  313.1 2.1 copy.27
  315.2 1.1 fusion.6
  317.2 11.7 %cholesky.261 = f32[128,128]{1,0:T(8,128)S(1)} custom-call(f32[128,128]{1,0:T(8,128)S(1)} %cholesky.318), custom_call_target="Cholesky" | custom-call | tf_op jit(solution)/shard_map/jit(cholesky)/cholesky | solution.py:60
  329.0 9.8 %custom-call.27 = f32[1,128,128]{1,2,0:T(8,128)S(1)} custom-call(f32[1,128,128]{2,1,0:T(8,128)S(1)} %get-tuple-element.49), custom_call_target="InvertDiagBlocksLowerTriangular" | custom-call | tf_op jit(solution)/shard_map/jit(cholesky)/cholesky | solution.py:60
  338.8 1.2 constant_dynamic-update-slice_fusion.1
  339.9 1.2 convolution_subtract_fusion.6
  341.1 11.7 %cholesky.280 = f32[128,128]{1,0:T(8,128)S(1)} custom-call(f32[128,128]{1,0:T(8,128)S(1)} %cholesky.322), custom_call_target="Cholesky" | custom-call | tf_op jit(solution)/shard_map/jit(cholesky)/cholesky | solution.py:60
  354.2 10.2 %custom-call.28 = f32[1,128,128]{1,2,0:T(8,128)S(1)} custom-call(f32[1,128,128]{2,1,0:T(8,128)S(1)} %get-tuple-element.46), custom_call_target="InvertDiagBlocksLowerTriangular" | custom-call | tf_op jit(solution)/shard_map/jit(cholesky)/cholesky | solution.py:60
  364.7 1.1 convolution_subtract_fusion.8
  365.8 11.7 %cholesky.299 = f32[128,128]{1,0:T(8,128)S(1)} custom-call(f32[128,128]{1,0:T(8,128)S(1)} %convolution_subtract_fusion.8), custom_call_target="Cholesky" | custom-call | tf_op jit(solution)/shard_map/jit(cholesky)/cholesky | solution.py:60
  381.1 8.6 %while.5 = (s32[]{:T(128)}, f32[384,384]{1,0:T(8,128)}, s32[3,2]{0,1:T(2,128)S(1)}, f32[3,128,128]{2,1,0:T(8,128)S(1)}, s32[]{:T(128)}) while((s32[]{:T(128)}, f32[384,384]{1,0:T(8,128)}, s32[3,2]{0,1:T(2,128)S(1)}, f32[3,128,128]{2,1,0:T(8,128)S(1)}, s32[]{:T(128)}) %tuple.65), condition=%wide.while_cond.clone, body=%wide.while_body.clone.sunk | while | flops 2 | bytes 131181 | solution.py:61
  381.7 2.2 bitcast_dynamic-update-slice_fusion.5
  384.6 2.2 bitcast_dynamic-update-slice_fusion.5
  387.5 2.2 bitcast_dynamic-update-slice_fusion.5
  389.7 29.5 %custom-call.29 = f32[3,128,128]{1,2,0:T(8,128)S(1)} custom-call(f32[3,128,128]{2,1,0:T(8,128)S(1)} %get-tuple-element.22), custom_call_target="InvertDiagBlocksLowerTriangular" | custom-call | tf_op jit(solution)/shard_map/triangular_solve/custom-call.2 | solution.py:61
  419.9 1.3 convolution_subtract_fusion.3
  421.2 1.2 fusion.78
  422.5 1.7 convolution_subtract_fusion.2
  424.2 1.2 fusion.76
  426.3 2.5 fusion.122
  429.0 2.1 fusion.38
  431.1 125.0 %all-reduce.4.cloned.1.call-done = f32[384,384]{1,0:T(8,128)} async-done(((f32[384,384]{1,0:T(8,128)}), f32[384,384]{1,0:T(8,128)}) %all-reduce.4.cloned.1.call-update) | async-done | bytes 589840 | tf_op jit(solution)/shard_map/psum | solution.py:70
  556.0 2.5 fusion
  558.6 1.5 fusion.34
  560.1 1.0 copy.32
  561.1 3.4 gather_fusion
  564.5 3.3 fusion.21
  567.8 2.2 fusion.114
  571.1 1.7 select_reduce_fusion.1
  573.3 1.8 convolution_multiply_fusion.1
  575.1 2.2 fusion.3
  577.3 1.4 fusion.123
  578.7 1.3 convolution_bitcast_fusion
  580.0 127.6 %all-reduce.6.cloned.1.call-done = f32[384,384]{1,0:T(8,128)} async-done(((f32[384,384]{1,0:T(8,128)}), f32[384,384]{1,0:T(8,128)}) %all-reduce.6.cloned.1.call-update) | async-done | bytes 589840 | tf_op jit(solution)/shard_map/psum | solution.py:70
  707.6 2.4 fusion.1
  710.0 1.5 fusion.36
  711.7 3.7 gather_fusion.1
  715.4 2.1 fusion.14
  717.5 1.3 fusion.116
  721.1 1.3 convolution_add_fusion
  (85 shorter events, 21.7 us)
Async XLA Ops:
  6.5 422.5 %copy-start = (f32[384,384]{1,0:T(8,128)S(1)}, f32[384,384]{1,0:T(8,128)}, u32[]{:S(2)}) copy-start(f32[384,384]{1,0:T(8,128)} %param.8) | copy-start | bytes 1769476
  6.5 13.8 %reduce-scatter.3.cloned.1.call-start = ((), (), s32[]{:S(2)}) async-start(), calls=%async_computation.2 | async-start | bytes 884736 | tf_op jit(solution)/shard_map/reduce_scatter | solution.py:45
  9.1 94.9 %all-gather.5.cloned.1.call-start = ((), (), s32[]{:S(2)}) async-start(), calls=%async_computation.6 | async-start | bytes 5013504 | tf_op jit(solution)/shard_map/all_gather | solution.py:46
  20.4 200.5 %reduce-scatter.5.cloned.1.call-start = ((), (), s32[]{:S(2)}) async-start(), calls=%async_computation.3 | async-start | bytes 884736 | tf_op jit(solution)/shard_map/reduce_scatter | solution.py:45
  110.7 101.2 %copy-start.2 = (f32[128,384]{1,0:T(8,128)S(1)}, f32[128,384]{1,0:T(8,128)}, u32[]{:S(2)}) copy-start(f32[128,384]{1,0:T(8,128)} %param.6) | copy-start | bytes 589828
  110.8 0.8 copy-start.5
  214.1 90.3 %all-gather.7.cloned.1.call-start = ((), (), s32[]{:S(2)}) async-start(), calls=%async_computation.7 | async-start | bytes 5013504 | tf_op jit(solution)/shard_map/all_gather | solution.py:46
  220.9 335.2 %all-reduce.4.cloned.1.call-start = ((), (), s32[]{:S(2)}) async-start(), calls=%async_computation.4 | async-start | bytes 1179648 | tf_op jit(solution)/shard_map/psum | solution.py:70
  316.3 0.8 copy-start.4
  419.2 0.7 copy-start.6
  425.4 130.6 %copy-start.1 = (f32[128,384]{1,0:T(8,128)}, f32[128,384]{1,0:T(8,128)S(1)}, u32[]{:S(2)}) copy-start(f32[128,384]{1,0:T(8,128)S(1)} %fusion.76) | copy-start | bytes 589828
  428.7 278.9 %all-reduce.6.cloned.1.call-start = ((), (), s32[]{:S(2)}) async-start(), calls=%async_computation.5 | async-start | bytes 1179648 | tf_op jit(solution)/shard_map/psum | solution.py:70
  711.5 8.8 %copy-start.3 = (f32[128,384]{1,0:T(8,128)S(1)}, f32[128,384]{1,0:T(8,128)}, u32[]{:S(2)}) copy-start(f32[128,384]{1,0:T(8,128)} %param.6) | copy-start | bytes 589828
Sparse Core Ops, SparseCore 0:
  9.6 10.6 reduce-scatter.2
  23.1 80.8 all-gather.4
  214.2 6.6 reduce-scatter.4
  223.5 80.8 all-gather.6
  428.9 127.1 all-reduce.3
  578.9 128.7 all-reduce.5
